TPU v7x, 256 devices: a whole 4x4x8 slice. The times are simulated.
256 devices in a mesh: gx: 8 (over z), gy: 4 (over x), gz: 8 (over y, core).
Axes of the slice: x: 4, y: 4, z: 8, core: 2. Of those that a mesh axis runs over, the one named last changes fastest.
Arguments:
- grads: float32 [256, 1, 1048576], P(('gx', 'gy', 'gz')), may hold values from -650 to 650
- loss_scale: float32 [], replicated, may hold values from 8 to 64
Outputs:
- clipped: float32 [1, 1048576], P(None, ('gx', 'gy', 'gz'))
- grad_norm: float32 [], replicated
All inputs are finite; a program needn't handle non-finite values.
Results may differ from a plain program's by a relative error of at most 0.00002.
Values sent between devices are 32-bit elements; how exact they have to be, the bound alone decides.
No kernel may reach another device: no remote copies, remote signals or barrier semaphores. Data moves between devices by JAX's collectives and lax.ppermute only.
A program may use at most 64 MiB of HBM per device.

v0:
```python
import jax
import jax.numpy as jnp
from jax import lax
from jax.sharding import Mesh
from jax.sharding import PartitionSpec as P

GX_GY_GZ = ("gx", "gy", "gz_0", "gz_1")


def cut_along(array, dim, length):
    before, after = (array.shape[:dim], array.shape[dim + 1 :])
    return jnp.moveaxis(array.reshape(*before, length, -1, *after), dim, 0)


def sent_and_summed(array, axis, dim):
    length = lax.axis_size(axis)
    blocks = lax.all_to_all(cut_along(array, dim, length), axis, 0, 0, tiled=True)
    return jnp.sum(blocks, axis=0)


def sum_in_two_steps(array, axes, dim):
    far, near = axes
    own = sent_and_summed(cut_along(array, dim, lax.axis_size(far)), near, dim + 1)
    return jnp.sum(lax.all_to_all(own, far, 0, 0, tiled=True), axis=0)


def sent_to_all(array, axis):
    copies = jnp.broadcast_to(array, (lax.axis_size(axis), *array.shape))
    return lax.all_to_all(copies, axis, split_axis=0, concat_axis=0, tiled=True)


def over_copies(array, axis):
    return sent_to_all(array, axis).sum(axis=0)


def over_axes(array, axes):
    far, near = axes
    return over_copies(over_copies(array, near), far)


def per_device(grads, loss_scale):
    local = grads[0]
    entries = local.shape[0] * local.shape[1]
    mine = sum_in_two_steps(local, (("gx", "gy"), ("gz_0", "gz_1")), 1) / loss_scale
    square = over_axes(jnp.sum(mine * mine), (("gx", "gy"), ("gz_0", "gz_1")))
    grad_norm = jnp.sqrt(square)
    factor = jnp.minimum(1.0, 0.5 * jnp.sqrt(jnp.float32(entries)) / (grad_norm + 1e-06))
    return (mine * factor, grad_norm)


def solution(mesh):
    torus = Mesh(
        mesh.devices.reshape(mesh.shape["gx"], mesh.shape["gy"], 4, 2), ("gx", "gy", "gz_0", "gz_1")
    )
    placed = (P(GX_GY_GZ, None, None), P())
    return jax.shard_map(
        per_device, mesh=torus, in_specs=placed, out_specs=(P(None, GX_GY_GZ), P()), check_vma=False
    )
```

profile of v0, /device:TPU:1, one launch (start us, length us, event | category | flops | bytes accessed | tf_op | source)
XLA Modules:
  0.0 123.0 jit_solution(956699849181283893)
XLA Ops:
  0.6 6.0 %copy.13 = f32[1,1,256,4096]{3,2,1,0:T(8,128)S(1)} copy(f32[1,1,256,4096]{3,1,2,0:T(1,128)} %bitcast.12) | data formatting | bytes 8388608
  6.6 2.4 %copy.6 = f32[8,32,1,4096]{3,1,2,0:T(8,128)S(1)} copy(f32[8,32,1,4096]{3,0,1,2:T(8,128)S(1)} %bitcast.11) | data formatting | bytes 8388608 | tf_op jit(solution)/shard_map/transpose | solution.py:12
  9.0 55.1 %all_to_all.22 = f32[8,32,1,4096]{3,1,2,0:T(8,128)} all-to-all(f32[8,32,1,4096]{3,1,2,0:T(8,128)S(1)} %copy.6), channel_id=1, replica_groups=mesh['gx'=8,'gy'=4,'gz_0'=4,'gz_1'=2] {'gz_0','gz_1'}, dimensions={0} | all-to-all | bytes 8388608 | tf_op jit(solution)/shard_map/all_to_all | solution.py:17
  64.1 2.4 %reduce_sum.47 = f32[32,4096]{1,0:T(8,128)S(1)} reduce(f32[8,32,1,4096]{3,1,2,0:T(8,128)} %all_to_all.22, f32[]{:T(128)} %constant.0.clone.1), dimensions={0,2}, to_apply=%region_0.0 | reduce | flops 917504 | bytes 4718596 | tf_op jit(solution)/shard_map/reduce_sum | solution.py:18
  66.6 1.4 %reduce_sum.48 = f32[32,1,4096]{2,1,0:T(1,128)} reshape(f32[32,4096]{1,0:T(8,128)S(1)} %reduce_sum.47) | data formatting | bytes 1048576 | tf_op jit(solution)/shard_map/reduce_sum | solution.py:18
  68.0 10.5 %all-to-all-start.1 = ((f32[32,1,4096]{2,1,0:T(1,128)}), f32[32,1,4096]{2,1,0:T(1,128)S(1)}, u32[]{:S(2)}, u32[]{:S(2)}) async-start(f32[32,1,4096]{2,1,0:T(1,128)} %reduce_sum.48), calls=%async_computation.1 | async-start | bytes 1048576 | tf_op jit(solution)/shard_map/all_to_all | solution.py:24
  79.1 14.7 %all-to-all-done.1 = f32[32,1,4096]{2,1,0:T(1,128)S(1)} async-done(((f32[32,1,4096]{2,1,0:T(1,128)}), f32[32,1,4096]{2,1,0:T(1,128)S(1)}, u32[]{:S(2)}, u32[]{:S(2)}) %all-to-all-start.1) | async-done | bytes 524320 | tf_op jit(solution)/shard_map/all_to_all | solution.py:24
  93.7 0.4 reduce_sum.49
  94.1 0.6 multiply_reduce_fusion
  94.7 0.6 broadcast_in_dim.6
  95.4 10.5 %all_to_all.23 = f32[8,1,1]{2,1,0:T(1,128)S(1)} all-to-all(f32[8,1,1]{2,1,0:T(1,128)S(1)} %broadcast_in_dim.6), channel_id=1, replica_groups=mesh['gx'=8,'gy'=4,'gz_0'=4,'gz_1'=2] {'gz_0','gz_1'}, dimensions={0} | all-to-all | bytes 64 | tf_op jit(solution)/shard_map/all_to_all | solution.py:29
  105.9 0.6 reduce_sum.51
  106.5 0.7 broadcast_in_dim.7
  107.2 12.8 %all_to_all.24 = f32[32,1,1]{2,1,0:T(1,128)S(1)} all-to-all(f32[32,1,1]{2,1,0:T(1,128)S(1)} %broadcast_in_dim.7), channel_id=1, replica_groups=mesh['gx'=8,'gy'=4,'gz_0'=4,'gz_1'=2] {'gx','gy'}, dimensions={0} | all-to-all | bytes 256 | tf_op jit(solution)/shard_map/all_to_all | solution.py:29
  119.9 0.6 reduce_sum.52
  121.3 0.6 broadcast_multiply_fusion
Async XLA Ops:
  68.0 25.8 %all-to-all-start.1 = ((f32[32,1,4096]{2,1,0:T(1,128)}), f32[32,1,4096]{2,1,0:T(1,128)S(1)}, u32[]{:S(2)}, u32[]{:S(2)}) async-start(f32[32,1,4096]{2,1,0:T(1,128)} %reduce_sum.48), calls=%async_computation.1 | async-start | bytes 1048576 | tf_op jit(solution)/shard_map/all_to_all | solution.py:24
where the time goes:
time: 123 us
  blocking collectives  78.4 us (64%)
  waiting for transfers between devices  14.7 us (12%)
  local copies, waits for them, and re-layouts  11.1 us (9%)
  starting transfers between devices  10.5 us (9%)
  other arithmetic  5.27 us (4%)
  between operations  3.18 us (3%)
    all_to_all x1, blocking collectives, sent_and_summed(): lax.all_to_all(cut_along(array, dim, length), axis, 0, 0, tiled=True)  55.1 us
    all_to_all x2, blocking collectives, sent_to_all(): return lax.all_to_all(copies, axis, split_axis=0, concat_axis=0, tiled=True)  23.3 us
    all_to_all x1, waiting for transfers between devices, sum_in_two_steps(): return jnp.sum(lax.all_to_all(own, far, 0, 0, tiled=True), axis=0)  14.7 us
    all_to_all x1, starting transfers between devices, sum_in_two_steps(): return jnp.sum(lax.all_to_all(own, far, 0, 0, tiled=True), axis=0)  10.5 us
    unnamed x1, local copies, waits for them, and re-layouts  5.98 us
  transfers between devices with their start and end apart: 1, of which 1 were waited for; matrix products, arithmetic and copies ran while one was open for 0% of the time, Pallas kernels for 0%

commit v1 on v0

v1 whole, which is shorter than its diff:
```python
import jax
import jax.numpy as jnp
from jax import lax
from jax.experimental import pallas as pl
from jax.experimental.pallas import tpu as pltpu
from jax.sharding import Mesh
from jax.sharding import PartitionSpec as P

Z, X, Y, CORES = 8, 4, 4, 2
DEVICES = Z * X * Y * CORES
HALF = DEVICES // CORES
ROWS, LANES = 32, 128
FIRST, SECOND = 8, 16


def device(z, x, y, core):
    return ((z * X + x) * Y + y) * CORES + core


def place(core, major, low, high, minor):
    if core == 0:
        return (2 * high + low, major, minor)
    return ((2 * high + low + 1) % Z, minor, major)


def groups(first):
    found = []
    for core in range(CORES):
        if first:
            for minor in range(4):
                for high in range(4):
                    found.append(
                        [device(*place(core, major, low, high, minor), core) for major in range(4) for low in range(2)]
                    )
        else:
            for major in range(4):
                for low in range(2):
                    found.append(
                        [device(*place(core, major, low, high, minor), core) for high in range(4) for minor in range(4)]
                    )
    return found


def copy_blocks(source, target, sem, core):
    def start(step, carry):
        major = step // 8
        low = (step // 4) % 2
        high = step % 4
        shifted = 2 * high + low

        @pl.when(core == 0)
        def _():
            pltpu.make_async_copy(source.at[shifted, major, :, 0], target.at[step], sem).start()

        @pl.when(core == 1)
        def _():
            pltpu.make_async_copy(source.at[(shifted + 1) % Z, :, major, 1], target.at[step], sem).start()

        return carry

    lax.fori_loop(0, HALF // 4, start, 0, unroll=True)
    pltpu.make_async_copy(target, target, sem).wait()


def pack(core_ref, source, target, sem):
    copy_blocks(source, target, sem, core_ref[0])


def packed(local, core):
    return pl.pallas_call(
        pack,
        out_shape=pltpu.VMEM((HALF // 4, 4, ROWS, LANES), jnp.float32),
        in_specs=[pl.BlockSpec(memory_space=pltpu.SMEM), pl.BlockSpec(memory_space=pltpu.HBM)],
        out_specs=pl.BlockSpec(memory_space=pltpu.VMEM),
        scratch_shapes=[pltpu.SemaphoreType.DMA],
        name="pack",
    )(core.reshape(1), local)


def unscale(loss_scale, parts, unscaled, squares):
    own = jnp.sum(parts[...], axis=0) / loss_scale[0]
    unscaled[...] = own
    squares[...] = jnp.broadcast_to(jnp.sum(own * own, axis=0, keepdims=True)[None], squares.shape)


def clip(unscaled, squares, clipped, norm):
    grad_norm = jnp.sqrt(jnp.sum(squares[...].reshape(DEVICES, LANES), keepdims=True))
    factor = jnp.minimum(1.0, 0.5 * jnp.sqrt(jnp.float32(DEVICES * ROWS * LANES)) / (grad_norm + 1e-06))
    clipped[...] = unscaled[...] * factor
    norm[...] = grad_norm


def per_device(grads, loss_scale):
    local = grads.reshape(Z, X, Y, CORES, ROWS, LANES)
    core = lax.axis_index("d") % CORES
    sent = packed(local, 1 - core)
    kept = packed(local, core)
    received = lax.ppermute(sent, "d", [(i, i ^ 1) for i in range(DEVICES)])
    chip = (kept + received).reshape(FIRST, SECOND * ROWS, LANES)
    first = lax.all_to_all(chip, "d", 0, 0, axis_index_groups=groups(True), tiled=True)
    first = jnp.sum(first, axis=0).reshape(SECOND, ROWS, LANES)
    second = lax.all_to_all(first, "d", 0, 0, axis_index_groups=groups(False), tiled=True)
    unscaled, squares = pl.pallas_call(
        unscale,
        out_shape=(
            jax.ShapeDtypeStruct((ROWS, LANES), jnp.float32),
            jax.ShapeDtypeStruct((DEVICES, 1, LANES), jnp.float32),
        ),
        in_specs=[pl.BlockSpec(memory_space=pltpu.SMEM), pl.BlockSpec(memory_space=pltpu.VMEM)],
        name="unscale",
    )(loss_scale.reshape(1), second)
    squares = lax.all_to_all(squares, "d", 0, 0, tiled=True)
    clipped, norm = pl.pallas_call(
        clip,
        out_shape=(
            jax.ShapeDtypeStruct((ROWS, LANES), jnp.float32),
            jax.ShapeDtypeStruct((1, 1), jnp.float32),
        ),
        name="clip",
    )(unscaled, squares)
    return (clipped.reshape(1, ROWS * LANES), norm.reshape(()))


def solution(mesh):
    flat = Mesh(mesh.devices.reshape(DEVICES), ("d",))
    return jax.shard_map(
        per_device,
        mesh=flat,
        in_specs=(P("d", None, None), P()),
        out_specs=(P(None, "d"), P()),
        check_vma=False,
    )
```

time: 123 us -> 80.9 us (0.66)
  blocking collectives: 78.4 us -> 43.1 us
  local copies, waits for them, and re-layouts: 11.1 us -> 0.69 us
  Pallas kernels: 0 us -> 7.9 us
  other arithmetic: 5.27 us -> 2.87 us
  between operations: 3.18 us -> 1.32 us
  waiting for transfers between devices: 14.7 us -> 13.4 us
    all_to_all x3 -> x2, blocking collectives: 78.4 us -> 43.1 us  [the longest x1 22.9 us: per_device(): lax.all_to_all(chip, 'd', 0, 0, axis_index_groups=groups(True), tiled=True)]
    pallas_call x0 -> x4, Pallas kernels: none -> 7.9 us  [the longest x2 4.47 us: packed(): pl.pallas_call(pack, out_shape=pltpu.VMEM((HALF // 4, 4, ROWS, LANES), jn...]
    unnamed x1 -> x2, local copies, waits for them, and re-layouts: 5.98 us -> 0.69 us
    reduce_sum x5 -> x1, other arithmetic: 4.65 us -> 0.8 us  [per_device(): first = jnp.sum(first, axis=0).reshape(SECOND, ROWS, LANES)]
    all_to_all x1, waiting for transfers between devices: 14.7 us -> 10.9 us  [per_device(): lax.all_to_all(first, 'd', 0, 0, axis_index_groups=groups(False), tiled=T...]
    ppermute x0 -> x1, starting transfers between devices: none -> 3.3 us  [per_device(): received = lax.ppermute(sent, 'd', [(i, i ^ 1) for i in range(DEVICES)])]
    all_to_all x1, starting transfers between devices: 10.5 us -> 7.76 us  [per_device(): lax.all_to_all(first, 'd', 0, 0, axis_index_groups=groups(False), tiled=T...]
    ppermute x0 -> x1, waiting for transfers between devices: none -> 2.55 us  [per_device(): received = lax.ppermute(sent, 'd', [(i, i ^ 1) for i in range(DEVICES)])]
  transfers between devices with their start and end apart: 1 -> 2, of which waited for: 1 -> 2; matrix products, arithmetic and copies ran while one was open for 0% -> 0% of each run, Pallas kernels for 0% -> 2%
where the time goes in v1:
time: 80.9 us; the launch traced here: 80.4 us
  blocking collectives  43.1 us (53%)
  waiting for transfers between devices  13.4 us (17%)
  starting transfers between devices  11.1 us (14%)
  Pallas kernels  7.9 us (10%)
  other arithmetic  2.87 us (4%)
  between operations  1.32 us (2%)
    all_to_all x1, blocking collectives, per_device(): lax.all_to_all(chip, 'd', 0, 0, axis_index_groups=groups(True), tiled=True)  22.9 us
    all_to_all x1, blocking collectives, per_device(): squares = lax.all_to_all(squares, 'd', 0, 0, tiled=True)  20.2 us
    all_to_all x1, waiting for transfers between devices, per_device(): lax.all_to_all(first, 'd', 0, 0, axis_index_groups=groups(False), tiled=T...  10.9 us
    all_to_all x1, starting transfers between devices, per_device(): lax.all_to_all(first, 'd', 0, 0, axis_index_groups=groups(False), tiled=T...  7.76 us
    pallas_call x2, Pallas kernels, packed(): pl.pallas_call(pack, out_shape=pltpu.VMEM((HALF // 4, 4, ROWS, LANES), jn...  4.47 us
    ppermute x1, starting transfers between devices, per_device(): received = lax.ppermute(sent, 'd', [(i, i ^ 1) for i in range(DEVICES)])  3.3 us
    ppermute x1, waiting for transfers between devices, per_device(): received = lax.ppermute(sent, 'd', [(i, i ^ 1) for i in range(DEVICES)])  2.55 us
    add x1, other arithmetic, per_device(): chip = (kept + received).reshape(FIRST, SECOND * ROWS, LANES)  2.07 us
  transfers between devices with their start and end apart: 2, of which 2 were waited for; matrix products, arithmetic and copies ran while one was open for 0% of the time, Pallas kernels for 2%

profile of v1, /device:TPU:1, one launch (start us, length us, event | category | flops | bytes accessed | tf_op | source)
XLA Modules:
  0.0 80.4 jit_solution(13606585976280891023)
XLA Ops:
  0.6 2.9 %pack.3 = f32[32,4,32,128]{3,2,1,0:T(8,128)} custom-call(s32[1]{0:T(128)} %bitcast.3.core_ref, f32[8,4,4,2,32,128]{5,4,3,2,1,0:T(8,128)} %bitcast.9), custom_call_target="tpu_custom_call" | custom-call | tf_op jit(solution)/shard_map/pack/pallas_call | solution.py:70
  3.5 3.3 %collective-permute-start = (f32[32,4,32,128]{3,2,1,0:T(8,128)}, f32[32,4,32,128]{3,2,1,0:T(8,128)}, u32[]{:S(2)}, u32[]{:S(2)}) collective-permute-start(f32[32,4,32,128]{3,2,1,0:T(8,128)} %pack.3), channel_id=1, source_target_pairs={{0,1},{1,0},{2,3},{3,2},{4,5},{5,4},{6,7},{7,6},{8,9},{9,8},{10,11... | collective-permute-start | bytes 6291464 | tf_op jit(solution)/shard_map/ppermute | solution.py:98
  6.8 1.6 %pack.2 = f32[32,4,32,128]{3,2,1,0:T(8,128)S(1)} custom-call(s32[1]{0:T(128)} %bitcast.1.core_ref, f32[8,4,4,2,32,128]{5,4,3,2,1,0:T(8,128)} %bitcast.10), custom_call_target="tpu_custom_call" | custom-call | tf_op jit(solution)/shard_map/pack/pallas_call | solution.py:70
  8.4 2.5 %collective-permute-done = f32[32,4,32,128]{3,2,1,0:T(8,128)} collective-permute-done((f32[32,4,32,128]{3,2,1,0:T(8,128)}, f32[32,4,32,128]{3,2,1,0:T(8,128)}, u32[]{:S(2)}, u32[]{:S(2)}) %collective-permute-start) | collective-permute-done | bytes 2097184 | tf_op jit(solution)/shard_map/ppermute | solution.py:98
  11.0 2.1 %add.8 = f32[32,4,32,128]{3,2,1,0:T(8,128)S(1)} add(f32[32,4,32,128]{3,2,1,0:T(8,128)S(1)} %pack.2, f32[32,4,32,128]{3,2,1,0:T(8,128)} %collective-permute-done) | non-fusion elementwise | flops 524288 | bytes 6291456 | tf_op jit(solution)/shard_map/add | solution.py:99
  13.0 22.9 %all_to_all.15 = f32[8,512,128]{2,1,0:T(8,128)S(1)} all-to-all(f32[8,512,128]{2,1,0:T(8,128)S(1)} %bitcast.11), channel_id=1, replica_groups={{0,32,8,40,16,48,24,56},{64,96,72,104,80,112,88,120},{128,160,136,168,1..., dimensions={0} | all-to-all | bytes 4194304 | tf_op jit(solution)/shard_map/all_to_all | solution.py:100
  36.0 0.8 %reduce_sum.9 = f32[512,128]{1,0:T(8,128)} reduce(f32[8,512,128]{2,1,0:T(8,128)S(1)} %all_to_all.15, f32[]{:T(128)} %constant.19.clone.1), dimensions={0}, to_apply=%region_0.1 | reduce | flops 458752 | bytes 2359300 | tf_op jit(solution)/shard_map/reduce_sum | solution.py:101
  36.8 7.8 %all-to-all-start.1 = ((f32[16,32,128]{2,1,0:T(8,128)}), f32[16,32,128]{2,1,0:T(8,128)S(1)}, u32[]{:S(2)}, u32[]{:S(2)}) async-start(f32[16,32,128]{2,1,0:T(8,128)} %bitcast.5), calls=%async_computation.1 | async-start | bytes 524288 | tf_op jit(solution)/shard_map/all_to_all | solution.py:102
  45.2 10.9 %all-to-all-done.1.parts = f32[16,32,128]{2,1,0:T(8,128)S(1)} async-done(((f32[16,32,128]{2,1,0:T(8,128)}), f32[16,32,128]{2,1,0:T(8,128)S(1)}, u32[]{:S(2)}, u32[]{:S(2)}) %all-to-all-start.1) | async-done | bytes 262176 | tf_op jit(solution)/shard_map/all_to_all | solution.py:102
  56.1 0.0 copy-start
  56.1 0.7 copy-done
  56.8 1.7 %unscale.1 = (f32[32,128]{1,0:T(8,128)}, f32[256,1,128]{2,1,0:T(1,128)}) custom-call(f32[1]{0:T(128)} %bitcast.8.loss_scale, f32[16,32,128]{2,1,0:T(8,128)} %copy-done), custom_call_target="tpu_custom_call" | custom-call | tf_op jit(solution)/shard_map/unscale/pallas_call | solution.py:103
  58.5 20.2 %all_to_all.16.squares = f32[256,1,128]{2,1,0:T(1,128)} all-to-all(f32[256,1,128]{2,1,0:T(1,128)} %get-tuple-element.7), channel_id=1, replica_groups=mesh['gx'=8,'gy'=4,'gz'=8] {'gx','gy','gz'}, dimensions={0} | all-to-all | bytes 262144 | tf_op jit(solution)/shard_map/all_to_all | solution.py:112
  78.7 1.7 %clip.1 = (f32[32,128]{1,0:T(8,128)}, f32[1,1]{1,0:T(1,128)}) custom-call(f32[32,128]{1,0:T(8,128)} %get-tuple-element.6.unscaled, f32[256,1,128]{2,1,0:T(1,128)} %all_to_all.16.squares), custom_call_target="tpu_custom_call" | custom-call | tf_op jit(solution)/shard_map/clip/pallas_call | solution.py:113
Async XLA Ops:
  3.5 7.4 %collective-permute-start = (f32[32,4,32,128]{3,2,1,0:T(8,128)}, f32[32,4,32,128]{3,2,1,0:T(8,128)}, u32[]{:S(2)}, u32[]{:S(2)}) collective-permute-start(f32[32,4,32,128]{3,2,1,0:T(8,128)} %pack.3), channel_id=1, source_target_pairs={{0,1},{1,0},{2,3},{3,2},{4,5},{5,4},{6,7},{7,6},{8,9},{9,8},{10,11... | collective-permute-start | bytes 6291464 | tf_op jit(solution)/shard_map/ppermute | solution.py:98
  36.8 19.3 %all-to-all-start.1 = ((f32[16,32,128]{2,1,0:T(8,128)}), f32[16,32,128]{2,1,0:T(8,128)S(1)}, u32[]{:S(2)}, u32[]{:S(2)}) async-start(f32[16,32,128]{2,1,0:T(8,128)} %bitcast.5), calls=%async_computation.1 | async-start | bytes 524288 | tf_op jit(solution)/shard_map/all_to_all | solution.py:102
  56.1 0.7 copy-start

commit v2 on v1

--- a/solution.py
+++ b/solution.py
@@ -41,44 +41,56 @@
     return found
 
 
-def copy_blocks(source, target, sem, core):
-    def start(step, carry):
-        major = step // 8
-        low = (step // 4) % 2
-        high = step % 4
-        shifted = 2 * high + low
+def copy_blocks(source, target, sem, partner):
+    core = (lax.axis_index("d") + partner) % CORES
+    for step in range(HALF // 4):
+        major, low, high = (step // 8, step // 4 % 2, step % 4)
+        chip = 2 * high + low
 
         @pl.when(core == 0)
         def _():
-            pltpu.make_async_copy(source.at[shifted, major, :, 0], target.at[step], sem).start()
+            pltpu.make_async_copy(source.at[chip, major, :, 0], target.at[step], sem).start()
 
         @pl.when(core == 1)
         def _():
-            pltpu.make_async_copy(source.at[(shifted + 1) % Z, :, major, 1], target.at[step], sem).start()
-
-        return carry
-
-    lax.fori_loop(0, HALF // 4, start, 0, unroll=True)
-    pltpu.make_async_copy(target, target, sem).wait()
+            pltpu.make_async_copy(source.at[(chip + 1) % Z, :, major, 1], target.at[step], sem).start()
 
 
-def pack(core_ref, source, target, sem):
-    copy_blocks(source, target, sem, core_ref[0])
+def pack_sent(source, sent, sem):
+    copy_blocks(source, sent, sem, 1)
+    pltpu.make_async_copy(sent, sent, sem).wait()
 
 
-def packed(local, core):
-    return pl.pallas_call(
-        pack,
-        out_shape=pltpu.VMEM((HALF // 4, 4, ROWS, LANES), jnp.float32),
-        in_specs=[pl.BlockSpec(memory_space=pltpu.SMEM), pl.BlockSpec(memory_space=pltpu.HBM)],
-        out_specs=pl.BlockSpec(memory_space=pltpu.VMEM),
-        scratch_shapes=[pltpu.SemaphoreType.DMA],
-        name="pack",
-    )(core.reshape(1), local)
+def pack_kept(loss_scale, source, kept, scale, sem):
+    copy_blocks(source, kept, sem, 0)
+    scale[...] = jnp.full(scale.shape, loss_scale[0])
+    pltpu.make_async_copy(kept, kept, sem).wait()
 
 
-def unscale(loss_scale, parts, unscaled, squares):
-    own = jnp.sum(parts[...], axis=0) / loss_scale[0]
+def packed(local, loss_scale):
+    blocks = pltpu.VMEM((HALF // 4, 4, ROWS, LANES), jnp.float32)
+    in_hbm, in_smem, in_vmem = (pl.BlockSpec(memory_space=m) for m in (pltpu.HBM, pltpu.SMEM, pltpu.VMEM))
+    options = dict(
+        scratch_shapes=[pltpu.SemaphoreType.DMA],
+        compiler_params=pltpu.CompilerParams(vmem_limit_bytes=4 << 20),
+    )
+    local = pltpu.with_memory_space_constraint(local, pltpu.HBM)
+    sent = pl.pallas_call(
+        pack_sent, out_shape=blocks, in_specs=[in_hbm], out_specs=in_vmem, name="pack_sent", **options
+    )(local)
+    kept, scale = pl.pallas_call(
+        pack_kept,
+        out_shape=(blocks, pltpu.VMEM((1, LANES), jnp.float32)),
+        in_specs=[in_smem, in_hbm],
+        out_specs=(in_vmem, in_vmem),
+        name="pack_kept",
+        **options,
+    )(loss_scale, local)
+    return sent, kept, scale
+
+
+def unscale(scale, parts, unscaled, squares):
+    own = jnp.sum(parts[...], axis=0) / scale[...]
     unscaled[...] = own
     squares[...] = jnp.broadcast_to(jnp.sum(own * own, axis=0, keepdims=True)[None], squares.shape)
 
@@ -92,9 +104,7 @@
 
 def per_device(grads, loss_scale):
     local = grads.reshape(Z, X, Y, CORES, ROWS, LANES)
-    core = lax.axis_index("d") % CORES
-    sent = packed(local, 1 - core)
-    kept = packed(local, core)
+    sent, kept, scale = packed(local, loss_scale.reshape(1))
     received = lax.ppermute(sent, "d", [(i, i ^ 1) for i in range(DEVICES)])
     chip = (kept + received).reshape(FIRST, SECOND * ROWS, LANES)
     first = lax.all_to_all(chip, "d", 0, 0, axis_index_groups=groups(True), tiled=True)
@@ -106,9 +116,9 @@
             jax.ShapeDtypeStruct((ROWS, LANES), jnp.float32),
             jax.ShapeDtypeStruct((DEVICES, 1, LANES), jnp.float32),
         ),
-        in_specs=[pl.BlockSpec(memory_space=pltpu.SMEM), pl.BlockSpec(memory_space=pltpu.VMEM)],
+        compiler_params=pltpu.CompilerParams(vmem_limit_bytes=2 << 20),
         name="unscale",
-    )(loss_scale.reshape(1), second)
+    )(scale, second)
     squares = lax.all_to_all(squares, "d", 0, 0, tiled=True)
     clipped, norm = pl.pallas_call(
         clip,
@@ -116,6 +126,7 @@
             jax.ShapeDtypeStruct((ROWS, LANES), jnp.float32),
             jax.ShapeDtypeStruct((1, 1), jnp.float32),
         ),
+        compiler_params=pltpu.CompilerParams(vmem_limit_bytes=2 << 20),
         name="clip",
     )(unscaled, squares)
     return (clipped.reshape(1, ROWS * LANES), norm.reshape(()))

time: 80.9 us -> 75.1 us (0.928)
  blocking collectives: 43.1 us -> 62.1 us
  waiting for transfers between devices: 13.4 us -> 1.67 us
  starting transfers between devices: 11.1 us -> 3.3 us
  Pallas kernels: 7.9 us -> 4.14 us
    all_to_all x0 -> x1, blocking collectives: none -> 19.1 us  [per_device(): lax.all_to_all(first, 'd', 0, 0, axis_index_groups=groups(False), tiled=T...]
    all_to_all x1 -> x0, waiting for transfers between devices: 10.9 us -> none  [per_device(): lax.all_to_all(first, 'd', 0, 0, axis_index_groups=groups(False), tiled=T...]
    all_to_all x1 -> x0, starting transfers between devices: 7.76 us -> none  [per_device(): lax.all_to_all(first, 'd', 0, 0, axis_index_groups=groups(False), tiled=T...]
    pallas_call x1, Pallas kernels: 1.7 us -> 0.1 us  [per_device(): pl.pallas_call(unscale, out_shape=(jax.ShapeDtypeStruct((ROWS, LANES), jn...]
    pallas_call x2, Pallas kernels: 4.47 us -> 3.17 us  [the longest x1 1.59 us: packed(): pl.pallas_call(pack_kept, out_shape=(blocks, pltpu.VMEM((1, LANES), jnp.f...]
    ppermute x1, waiting for transfers between devices: 2.55 us -> 1.67 us  [per_device(): received = lax.ppermute(sent, 'd', [(i, i ^ 1) for i in range(DEVICES)])]
    pallas_call x1, Pallas kernels: 1.73 us -> 0.87 us  [per_device(): pl.pallas_call(clip, out_shape=(jax.ShapeDtypeStruct((ROWS, LANES), jnp.f...]
  transfers between devices with their start and end apart: 2 -> 1, of which waited for: 2 -> 1; matrix products, arithmetic and copies ran while one was open for 0% -> 0% of each run, Pallas kernels for 2% -> 2%
where the time goes in v2:
time: 75.1 us; the launch traced here: 74.7 us
  blocking collectives  62.1 us (83%)
  Pallas kernels  4.14 us (6%)
  starting transfers between devices  3.3 us (4%)
  other arithmetic  2.19 us (3%)
  waiting for transfers between devices  1.67 us (2%)
  between operations  1.31 us (2%)
    all_to_all x1, blocking collectives, per_device(): lax.all_to_all(chip, 'd', 0, 0, axis_index_groups=groups(True), tiled=True)  22.9 us
    all_to_all x1, blocking collectives, per_device(): squares = lax.all_to_all(squares, 'd', 0, 0, tiled=True)  20.1 us
    all_to_all x1, blocking collectives, per_device(): lax.all_to_all(first, 'd', 0, 0, axis_index_groups=groups(False), tiled=T...  19.1 us
    ppermute x1, starting transfers between devices, per_device(): received = lax.ppermute(sent, 'd', [(i, i ^ 1) for i in range(DEVICES)])  3.3 us
    add x1, other arithmetic, per_device(): chip = (kept + received).reshape(FIRST, SECOND * ROWS, LANES)  2.07 us
    ppermute x1, waiting for transfers between devices, per_device(): received = lax.ppermute(sent, 'd', [(i, i ^ 1) for i in range(DEVICES)])  1.67 us
    pallas_call x1, Pallas kernels, packed(): pl.pallas_call(pack_kept, out_shape=(blocks, pltpu.VMEM((1, LANES), jnp.f...  1.59 us
    pallas_call x1, Pallas kernels, packed(): pl.pallas_call(pack_sent, out_shape=blocks, in_specs=[in_hbm], out_specs=...  1.58 us
  transfers between devices with their start and end apart: 1, of which 1 were waited for; matrix products, arithmetic and copies ran while one was open for 0% of the time, Pallas kernels for 2%

profile of v2, /device:TPU:1, one launch (start us, length us, event | category | flops | bytes accessed | tf_op | source)
XLA Modules:
  0.0 74.7 jit_solution(1138644551019039945)
XLA Ops:
  0.6 1.6 %pack_sent.1 = f32[32,4,32,128]{3,2,1,0:T(8,128)S(1)} custom-call(f32[8,4,4,2,32,128]{5,4,3,2,1,0:T(8,128)} %bitcast.7), custom_call_target="tpu_custom_call" | custom-call | tf_op jit(solution)/shard_map/pack_sent/pallas_call | solution.py:78
  2.2 3.3 %collective-permute-start = (f32[32,4,32,128]{3,2,1,0:T(8,128)S(1)}, f32[32,4,32,128]{3,2,1,0:T(8,128)}, u32[]{:S(2)}, u32[]{:S(2)}) collective-permute-start(f32[32,4,32,128]{3,2,1,0:T(8,128)S(1)} %pack_sent.1), channel_id=1, source_target_pairs={{0,1},{1,0},{2,3},{3,2},{4,5},{5,4},{6,7},{7,6},{8,9},{9,8},{10,11... | collective-permute-start | bytes 6291464 | tf_op jit(solution)/shard_map/ppermute | solution.py:108
  6.2 1.6 %pack_kept.1 = (f32[32,4,32,128]{3,2,1,0:T(8,128)S(1)}, f32[1,128]{1,0:T(1,128)S(1)}) custom-call(f32[1]{0:T(128)} %bitcast.6.loss_scale, f32[8,4,4,2,32,128]{5,4,3,2,1,0:T(8,128)} %bitcast.8), custom_call_target="tpu_custom_call" | custom-call | tf_op jit(solution)/shard_map/pack_kept/pallas_call | solution.py:81
  7.8 1.7 %collective-permute-done = f32[32,4,32,128]{3,2,1,0:T(8,128)} collective-permute-done((f32[32,4,32,128]{3,2,1,0:T(8,128)S(1)}, f32[32,4,32,128]{3,2,1,0:T(8,128)}, u32[]{:S(2)}, u32[]{:S(2)}) %collective-permute-start) | collective-permute-done | bytes 2097184 | tf_op jit(solution)/shard_map/ppermute | solution.py:108
  9.4 2.1 %add.3 = f32[32,4,32,128]{3,2,1,0:T(8,128)S(1)} add(f32[32,4,32,128]{3,2,1,0:T(8,128)S(1)} %get-tuple-element.9, f32[32,4,32,128]{3,2,1,0:T(8,128)} %collective-permute-done) | non-fusion elementwise | flops 524288 | bytes 6291456 | tf_op jit(solution)/shard_map/add | solution.py:109
  11.5 22.9 %all_to_all.15 = f32[8,512,128]{2,1,0:T(8,128)S(1)} all-to-all(f32[8,512,128]{2,1,0:T(8,128)S(1)} %bitcast.9), channel_id=1, replica_groups={{0,32,8,40,16,48,24,56},{64,96,72,104,80,112,88,120},{128,160,136,168,1..., dimensions={0} | all-to-all | bytes 4194304 | tf_op jit(solution)/shard_map/all_to_all | solution.py:110
  34.4 0.1 reduce_sum.9
  34.6 19.1 %all_to_all.16.parts = f32[16,32,128]{2,1,0:T(8,128)S(1)} all-to-all(f32[16,32,128]{2,1,0:T(8,128)S(1)} %bitcast.10), channel_id=1, replica_groups={{0,2,4,6,64,66,68,70,128,130,132,134,192,194,196,198},{32,34,36,38,96,9..., dimensions={0} | all-to-all | bytes 524288 | tf_op jit(solution)/shard_map/all_to_all | solution.py:112
  53.6 0.1 unscale.1
  53.7 20.1 %all_to_all.17.squares = f32[256,1,128]{2,1,0:T(1,128)S(1)} all-to-all(f32[256,1,128]{2,1,0:T(1,128)S(1)} %get-tuple-element.11), channel_id=1, replica_groups=mesh['gx'=8,'gy'=4,'gz'=8] {'gx','gy','gz'}, dimensions={0} | all-to-all | bytes 262144 | tf_op jit(solution)/shard_map/all_to_all | solution.py:122
  73.8 0.9 %clip.1 = (f32[32,128]{1,0:T(8,128)}, f32[1,1]{1,0:T(1,128)}) custom-call(f32[32,128]{1,0:T(8,128)S(1)} %get-tuple-element.10.unscaled, f32[256,1,128]{2,1,0:T(1,128)S(1)} %all_to_all.17.squares), custom_call_target="tpu_custom_call" | custom-call | tf_op jit(solution)/shard_map/clip/pallas_call | solution.py:123
Async XLA Ops:
  2.2 7.2 %collective-permute-start = (f32[32,4,32,128]{3,2,1,0:T(8,128)S(1)}, f32[32,4,32,128]{3,2,1,0:T(8,128)}, u32[]{:S(2)}, u32[]{:S(2)}) collective-permute-start(f32[32,4,32,128]{3,2,1,0:T(8,128)S(1)} %pack_sent.1), channel_id=1, source_target_pairs={{0,1},{1,0},{2,3},{3,2},{4,5},{5,4},{6,7},{7,6},{8,9},{9,8},{10,11... | collective-permute-start | bytes 6291464 | tf_op jit(solution)/shard_map/ppermute | solution.py:108

commit v3 on v2

--- a/solution.py
+++ b/solution.py
@@ -56,37 +56,49 @@
             pltpu.make_async_copy(source.at[(chip + 1) % Z, :, major, 1], target.at[step], sem).start()
 
 
-def pack_sent(source, sent, sem):
+def pack_sent(loss_scale, source, sent, scale, sem, scale_sem, scale_smem):
     copy_blocks(source, sent, sem, 1)
+    copy_scale = pltpu.make_async_copy(loss_scale, scale_smem, scale_sem)
+    copy_scale.start()
+    copy_scale.wait()
+    scale[...] = jnp.full(scale.shape, scale_smem[0])
     pltpu.make_async_copy(sent, sent, sem).wait()
 
 
-def pack_kept(loss_scale, source, kept, scale, sem):
+def pack_kept(source, kept, sem):
     copy_blocks(source, kept, sem, 0)
-    scale[...] = jnp.full(scale.shape, loss_scale[0])
     pltpu.make_async_copy(kept, kept, sem).wait()
 
 
 def packed(local, loss_scale):
     blocks = pltpu.VMEM((HALF // 4, 4, ROWS, LANES), jnp.float32)
-    in_hbm, in_smem, in_vmem = (pl.BlockSpec(memory_space=m) for m in (pltpu.HBM, pltpu.SMEM, pltpu.VMEM))
-    options = dict(
-        scratch_shapes=[pltpu.SemaphoreType.DMA],
-        compiler_params=pltpu.CompilerParams(vmem_limit_bytes=4 << 20),
-    )
+    in_hbm, in_vmem = (pl.BlockSpec(memory_space=m) for m in (pltpu.HBM, pltpu.VMEM))
+    params = pltpu.CompilerParams(vmem_limit_bytes=4 << 20)
+    sem = pltpu.SemaphoreType.DMA
     local = pltpu.with_memory_space_constraint(local, pltpu.HBM)
-    sent = pl.pallas_call(
-        pack_sent, out_shape=blocks, in_specs=[in_hbm], out_specs=in_vmem, name="pack_sent", **options
+    sent, scale = pl.pallas_call(
+        pack_sent,
+        out_shape=(blocks, pltpu.VMEM((1, LANES), jnp.float32)),
+        in_specs=[pl.BlockSpec(memory_space=pl.ANY), in_hbm],
+        out_specs=(in_vmem, in_vmem),
+        scratch_shapes=[sem, sem, pltpu.SMEM((1,), jnp.float32)],
+        compiler_params=params,
+        name="pack_sent",
+    )(loss_scale, local)
+    kept = pl.pallas_call(
+        pack_kept,
+        out_shape=blocks,
+        in_specs=[in_hbm],
+        out_specs=in_vmem,
+        scratch_shapes=[sem],
+        compiler_params=params,
+        name="pack_kept",
     )(local)
-    kept, scale = pl.pallas_call(
-        pack_kept,
-        out_shape=(blocks, pltpu.VMEM((1, LANES), jnp.float32)),
-        in_specs=[in_smem, in_hbm],
-        out_specs=(in_vmem, in_vmem),
-        name="pack_kept",
-        **options,
-    )(loss_scale, local)
     return sent, kept, scale
+
+
+def add_pair(kept, received, chip):
+    chip[...] = kept[...] + received[...]
 
 
 def unscale(scale, parts, unscaled, squares):
@@ -106,7 +118,13 @@
     local = grads.reshape(Z, X, Y, CORES, ROWS, LANES)
     sent, kept, scale = packed(local, loss_scale.reshape(1))
     received = lax.ppermute(sent, "d", [(i, i ^ 1) for i in range(DEVICES)])
-    chip = (kept + received).reshape(FIRST, SECOND * ROWS, LANES)
+    chip = pl.pallas_call(
+        add_pair,
+        out_shape=pltpu.VMEM(kept.shape, jnp.float32),
+        compiler_params=pltpu.CompilerParams(vmem_limit_bytes=4 << 20),
+        name="add_pair",
+    )(kept, pltpu.with_memory_space_constraint(received, pltpu.VMEM))
+    chip = chip.reshape(FIRST, SECOND * ROWS, LANES)
     first = lax.all_to_all(chip, "d", 0, 0, axis_index_groups=groups(True), tiled=True)
     first = jnp.sum(first, axis=0).reshape(SECOND, ROWS, LANES)
     second = lax.all_to_all(first, "d", 0, 0, axis_index_groups=groups(False), tiled=True)

time: 75.1 us -> 73.7 us (0.981)
  other arithmetic: 2.19 us -> 0.12 us
    add x1 -> x0, other arithmetic: 2.07 us -> none  [per_device(): chip = (kept + received).reshape(FIRST, SECOND * ROWS, LANES)]
    pallas_call x2 -> x3, Pallas kernels: 3.17 us -> 3.37 us  [the longest x1 1.59 us: packed(): pl.pallas_call(pack_sent, out_shape=(blocks, pltpu.VMEM((1, LANES), jnp.f...]
where the time goes in v3:
time: 73.7 us; the launch traced here: 73.3 us
  blocking collectives  62.1 us (84%)
  Pallas kernels  4.34 us (6%)
  starting transfers between devices  3.3 us (4%)
  waiting for transfers between devices  2.21 us (3%)
  between operations  1.3 us (2%)
    all_to_all x1, blocking collectives, per_device(): lax.all_to_all(chip, 'd', 0, 0, axis_index_groups=groups(True), tiled=True)  22.9 us
    all_to_all x1, blocking collectives, per_device(): squares = lax.all_to_all(squares, 'd', 0, 0, tiled=True)  20.1 us
    all_to_all x1, blocking collectives, per_device(): lax.all_to_all(first, 'd', 0, 0, axis_index_groups=groups(False), tiled=T...  19.1 us
    ppermute x1, starting transfers between devices, per_device(): received = lax.ppermute(sent, 'd', [(i, i ^ 1) for i in range(DEVICES)])  3.3 us
    ppermute x1, waiting for transfers between devices, per_device(): received = lax.ppermute(sent, 'd', [(i, i ^ 1) for i in range(DEVICES)])  2.21 us
    pallas_call x1, Pallas kernels, packed(): pl.pallas_call(pack_sent, out_shape=(blocks, pltpu.VMEM((1, LANES), jnp.f...  1.59 us
    pallas_call x1, Pallas kernels, packed(): pl.pallas_call(pack_kept, out_shape=blocks, in_specs=[in_hbm], out_specs=...  1.57 us
  transfers between devices with their start and end apart: 1, of which 1 were waited for; matrix products, arithmetic and copies ran while one was open for 0% of the time, Pallas kernels for 2%

profile of v3, /device:TPU:1, one launch (start us, length us, event | category | flops | bytes accessed | tf_op | source)
XLA Modules:
  0.0 73.3 jit_solution(493650363706245459)
XLA Ops:
  1.3 1.6 %pack_sent.1 = (f32[32,4,32,128]{3,2,1,0:T(8,128)S(1)}, f32[1,128]{1,0:T(1,128)S(1)}) custom-call(f32[1]{0:T(128)} %bitcast.6.loss_scale, f32[8,4,4,2,32,128]{5,4,3,2,1,0:T(8,128)} %bitcast.8), custom_call_target="tpu_custom_call" | custom-call | tf_op jit(solution)/shard_map/pack_sent/pallas_call | solution.py:79
  2.9 3.3 %collective-permute-start = (f32[32,4,32,128]{3,2,1,0:T(8,128)S(1)}, f32[32,4,32,128]{3,2,1,0:T(8,128)S(1)}, u32[]{:S(2)}, u32[]{:S(2)}) collective-permute-start(f32[32,4,32,128]{3,2,1,0:T(8,128)S(1)} %get-tuple-element.9), channel_id=1, source_target_pairs={{0,1},{1,0},{2,3},{3,2},{4,5},{5,4},{6,7},{7,6},{8,9},{9,8},{10,11... | collective-permute-start | bytes 6291464 | tf_op jit(solution)/shard_map/ppermute | solution.py:120
  6.2 1.6 %pack_kept.1.kept = f32[32,4,32,128]{3,2,1,0:T(8,128)S(1)} custom-call(f32[8,4,4,2,32,128]{5,4,3,2,1,0:T(8,128)} %bitcast.9), custom_call_target="tpu_custom_call" | custom-call | tf_op jit(solution)/shard_map/pack_kept/pallas_call | solution.py:88
  7.8 2.2 %collective-permute-done.received = f32[32,4,32,128]{3,2,1,0:T(8,128)S(1)} collective-permute-done((f32[32,4,32,128]{3,2,1,0:T(8,128)S(1)}, f32[32,4,32,128]{3,2,1,0:T(8,128)S(1)}, u32[]{:S(2)}, u32[]{:S(2)}) %collective-permute-start) | collective-permute-done | bytes 2097184 | tf_op jit(solution)/shard_map/ppermute | solution.py:120
  10.0 0.2 add_pair.1
  10.2 22.9 %all_to_all.15 = f32[8,512,128]{2,1,0:T(8,128)S(1)} all-to-all(f32[8,512,128]{2,1,0:T(8,128)S(1)} %bitcast.7), channel_id=1, replica_groups={{0,32,8,40,16,48,24,56},{64,96,72,104,80,112,88,120},{128,160,136,168,1..., dimensions={0} | all-to-all | bytes 4194304 | tf_op jit(solution)/shard_map/all_to_all | solution.py:128
  33.1 0.1 reduce_sum.9
  33.2 19.1 %all_to_all.16.parts = f32[16,32,128]{2,1,0:T(8,128)S(1)} all-to-all(f32[16,32,128]{2,1,0:T(8,128)S(1)} %bitcast.10), channel_id=1, replica_groups={{0,2,4,6,64,66,68,70,128,130,132,134,192,194,196,198},{32,34,36,38,96,9..., dimensions={0} | all-to-all | bytes 524288 | tf_op jit(solution)/shard_map/all_to_all | solution.py:130
  52.3 0.1 unscale.1
  52.4 20.1 %all_to_all.17.squares = f32[256,1,128]{2,1,0:T(1,128)S(1)} all-to-all(f32[256,1,128]{2,1,0:T(1,128)S(1)} %get-tuple-element.11), channel_id=1, replica_groups=mesh['gx'=8,'gy'=4,'gz'=8] {'gx','gy','gz'}, dimensions={0} | all-to-all | bytes 262144 | tf_op jit(solution)/shard_map/all_to_all | solution.py:140
  72.5 0.9 %clip.1 = (f32[32,128]{1,0:T(8,128)}, f32[1,1]{1,0:T(1,128)}) custom-call(f32[32,128]{1,0:T(8,128)S(1)} %get-tuple-element.10.unscaled, f32[256,1,128]{2,1,0:T(1,128)S(1)} %all_to_all.17.squares), custom_call_target="tpu_custom_call" | custom-call | tf_op jit(solution)/shard_map/clip/pallas_call | solution.py:141
Async XLA Ops:
  2.9 7.1 %collective-permute-start = (f32[32,4,32,128]{3,2,1,0:T(8,128)S(1)}, f32[32,4,32,128]{3,2,1,0:T(8,128)S(1)}, u32[]{:S(2)}, u32[]{:S(2)}) collective-permute-start(f32[32,4,32,128]{3,2,1,0:T(8,128)S(1)} %get-tuple-element.9), channel_id=1, source_target_pairs={{0,1},{1,0},{2,3},{3,2},{4,5},{5,4},{6,7},{7,6},{8,9},{9,8},{10,11... | collective-permute-start | bytes 6291464 | tf_op jit(solution)/shard_map/ppermute | solution.py:120

commit v4 on v3

v4 whole, which is shorter than its diff:
```python
import jax
import jax.numpy as jnp
from jax import lax
from jax.experimental import pallas as pl
from jax.experimental.pallas import tpu as pltpu
from jax.sharding import Mesh
from jax.sharding import PartitionSpec as P

Z, X, Y, CORES = 8, 4, 4, 2
DEVICES = Z * X * Y * CORES
HALF = DEVICES // CORES
ROWS, LANES = 32, 128
PAIRS = [(i, i ^ 1) for i in range(DEVICES)]


def device(major, low, minor, high, core):
    z = 2 * high + low
    x, y = (major, minor)
    if core == 1:
        z, x, y = ((z + 1) % Z, minor, major)
    return ((z * X + x) * Y + y) * CORES + core


def along_major_and_low():
    return [
        [device(major, low, minor, high, core) for major in range(4) for low in range(2)]
        for core in range(CORES)
        for minor in range(4)
        for high in range(4)
    ]


def along_minor():
    return [
        [device(major, low, minor, high, core) for minor in range(4)]
        for core in range(CORES)
        for major in range(4)
        for low in range(2)
        for high in range(4)
    ]


def along_high():
    return [
        [device(major, low, minor, high, core) for high in range(4)]
        for core in range(CORES)
        for major in range(4)
        for low in range(2)
        for minor in range(4)
    ]


def pairs_of_planes():
    plane = X * Y * CORES
    return [list(range(2 * high * plane, 2 * (high + 1) * plane)) for high in range(4)]


def exchanged(blocks, groups):
    return lax.all_to_all(blocks, "d", 0, 0, axis_index_groups=groups, tiled=True)


def copy_blocks(source, target, sem, partner):
    core = (lax.axis_index("d") + partner) % CORES

    @pl.when(core == 0)
    def _():
        for z in range(Z):
            for x in range(X):
                pltpu.make_async_copy(source.at[z, x, :, 0], target.at[2 * x + z % 2, :, z // 2], sem).start()

    @pl.when(core == 1)
    def _():
        for z in range(Z):
            for y in range(Y):
                pltpu.make_async_copy(
                    source.at[(z + 1) % Z, :, y, 1], target.at[2 * y + z % 2, :, z // 2], sem
                ).start()


def pack_sent(loss_scale, source, sent, scale, sem, scale_sem, scale_smem):
    copy_blocks(source, sent, sem, 1)
    copy_scale = pltpu.make_async_copy(loss_scale, scale_smem, scale_sem)
    copy_scale.start()
    copy_scale.wait()
    scale[...] = jnp.full(scale.shape, scale_smem[0])
    pltpu.make_async_copy(sent, sent, sem).wait()


def pack_kept(source, kept, sem):
    copy_blocks(source, kept, sem, 0)
    pltpu.make_async_copy(kept, kept, sem).wait()


def packed(local, loss_scale):
    blocks = pltpu.VMEM((8, 4, 4, ROWS, LANES), jnp.float32)
    in_hbm, in_vmem = (pl.BlockSpec(memory_space=m) for m in (pltpu.HBM, pltpu.VMEM))
    params = pltpu.CompilerParams(vmem_limit_bytes=4 << 20)
    sem = pltpu.SemaphoreType.DMA
    local = pltpu.with_memory_space_constraint(local, pltpu.HBM)
    sent, scale = pl.pallas_call(
        pack_sent,
        out_shape=(blocks, pltpu.VMEM((1, LANES), jnp.float32)),
        in_specs=[pl.BlockSpec(memory_space=pl.ANY), in_hbm],
        out_specs=(in_vmem, in_vmem),
        scratch_shapes=[sem, sem, pltpu.SMEM((1,), jnp.float32)],
        compiler_params=params,
        name="pack_sent",
    )(loss_scale, local)
    kept = pl.pallas_call(
        pack_kept,
        out_shape=blocks,
        in_specs=[in_hbm],
        out_specs=in_vmem,
        scratch_shapes=[sem],
        compiler_params=params,
        name="pack_kept",
    )(local)
    return sent, kept, scale


def add_pair(kept, received, chip):
    chip[...] = kept[...] + received[...]


def add_minor(parts, copies):
    copies[...] = jnp.broadcast_to(jnp.sum(parts[...], axis=0, keepdims=True), copies.shape)


def unscale(scale, parts, unscaled, squares):
    index = lax.axis_index("d")
    high = (index // (X * Y * CORES) + Z - index % CORES) % Z // 2
    blocks = jnp.sum(parts[...], axis=0) / scale[...]
    unscaled[...] = jnp.sum(parts[:, pl.ds(high * ROWS, ROWS)], axis=0) / scale[...]
    squares[...] = jnp.broadcast_to(jnp.sum(blocks * blocks, axis=0, keepdims=True)[None], squares.shape)


def clip(unscaled, squares, clipped, norm):
    grad_norm = jnp.sqrt(jnp.sum(squares[...].reshape(-1, LANES), keepdims=True))
    factor = jnp.minimum(1.0, 0.5 * jnp.sqrt(jnp.float32(DEVICES * ROWS * LANES)) / (grad_norm + 1e-06))
    clipped[...] = unscaled[...] * factor
    norm[...] = grad_norm


def called(kernel, *args, out, mib=2):
    return pl.pallas_call(
        kernel,
        out_shape=out,
        compiler_params=pltpu.CompilerParams(vmem_limit_bytes=mib << 20),
        name=kernel.__name__,
    )(*args)


def per_device(grads, loss_scale):
    sent, kept, scale = packed(grads.reshape(Z, X, Y, CORES, ROWS, LANES), loss_scale.reshape(1))
    received = pltpu.with_memory_space_constraint(lax.ppermute(sent, "d", PAIRS), pltpu.VMEM)
    chip = called(add_pair, kept, received, out=pltpu.VMEM(kept.shape, jnp.float32), mib=4)
    blocks = exchanged(chip.reshape(8, 16 * ROWS, LANES), along_major_and_low())
    blocks = jnp.sum(blocks, axis=0)
    blocks = exchanged(blocks.reshape(4, 4 * ROWS, LANES), along_minor())
    copies = called(add_minor, blocks, out=pltpu.VMEM((4, 4 * ROWS, LANES), jnp.float32))
    blocks = exchanged(copies, along_high())
    unscaled, squares = called(
        unscale,
        scale,
        blocks,
        out=(
            jax.ShapeDtypeStruct((ROWS, LANES), jnp.float32),
            jax.ShapeDtypeStruct((2 * X * Y * CORES, 1, LANES), jnp.float32),
        ),
    )
    clipped, norm = called(
        clip,
        unscaled,
        exchanged(squares, pairs_of_planes()),
        out=(jax.ShapeDtypeStruct((ROWS, LANES), jnp.float32), jax.ShapeDtypeStruct((1, 1), jnp.float32)),
    )
    return (clipped.reshape(1, ROWS * LANES), norm.reshape(()))


def solution(mesh):
    flat = Mesh(mesh.devices.reshape(DEVICES), ("d",))
    return jax.shard_map(
        per_device,
        mesh=flat,
        in_specs=(P("d", None, None), P()),
        out_specs=(P(None, "d"), P()),
        check_vma=False,
    )
```

time: 73.7 us -> 72.6 us (0.985)
  blocking collectives: 62.1 us -> 61 us
    all_to_all x3 -> x4, blocking collectives: 62.1 us -> 61 us  [exchanged(): lax.all_to_all(blocks, 'd', 0, 0, axis_index_groups=groups, tiled=True)]
where the time goes in v4:
time: 72.6 us; the launch traced here: 72.2 us
  blocking collectives  61 us (84%)
  Pallas kernels  4.2 us (6%)
  starting transfers between devices  3.31 us (5%)
  waiting for transfers between devices  2.21 us (3%)
  between operations  1.31 us (2%)
    all_to_all x4, blocking collectives, exchanged(): lax.all_to_all(blocks, 'd', 0, 0, axis_index_groups=groups, tiled=True)  61 us
    ppermute x1, starting transfers between devices, per_device(): lax.ppermute(sent, 'd', PAIRS)  3.31 us
    ppermute x1, waiting for transfers between devices, per_device(): lax.ppermute(sent, 'd', PAIRS)  2.21 us
    pallas_call x1, Pallas kernels, packed(): pl.pallas_call(pack_sent, out_shape=(blocks, pltpu.VMEM((1, LANES), jnp.f...  1.58 us
    pallas_call x1, Pallas kernels, packed(): pl.pallas_call(pack_kept, out_shape=blocks, in_specs=[in_hbm], out_specs=...  1.57 us
  transfers between devices with their start and end apart: 1, of which 1 were waited for; matrix products, arithmetic and copies ran while one was open for 0% of the time, Pallas kernels for 2%

profile of v4, /device:TPU:1, one launch (start us, length us, event | category | flops | bytes accessed | tf_op | source)
XLA Modules:
  0.0 72.2 jit_solution(16248186137653382388)
XLA Ops:
  1.3 1.6 %pack_sent.1 = (f32[8,4,4,32,128]{4,3,2,1,0:T(8,128)S(1)}, f32[1,128]{1,0:T(1,128)S(1)}) custom-call(f32[1]{0:T(128)} %bitcast.6.loss_scale, f32[8,4,4,2,32,128]{5,4,3,2,1,0:T(8,128)} %bitcast.8), custom_call_target="tpu_custom_call" | custom-call | tf_op jit(solution)/shard_map/pack_sent/pallas_call | solution.py:100
  2.9 3.3 %collective-permute-start = (f32[8,4,4,32,128]{4,3,2,1,0:T(8,128)S(1)}, f32[8,4,4,32,128]{4,3,2,1,0:T(8,128)S(1)}, u32[]{:S(2)}, u32[]{:S(2)}) collective-permute-start(f32[8,4,4,32,128]{4,3,2,1,0:T(8,128)S(1)} %get-tuple-element.9), channel_id=1, source_target_pairs={{0,1},{1,0},{2,3},{3,2},{4,5},{5,4},{6,7},{7,6},{8,9},{9,8},{10,11... | collective-permute-start | bytes 6291464 | tf_op jit(solution)/shard_map/ppermute | solution.py:155
  6.2 1.6 %pack_kept.1.kept = f32[8,4,4,32,128]{4,3,2,1,0:T(8,128)S(1)} custom-call(f32[8,4,4,2,32,128]{5,4,3,2,1,0:T(8,128)} %bitcast.9), custom_call_target="tpu_custom_call" | custom-call | tf_op jit(solution)/shard_map/pack_kept/pallas_call | solution.py:109
  7.7 2.2 %collective-permute-done.received = f32[8,4,4,32,128]{4,3,2,1,0:T(8,128)S(1)} collective-permute-done((f32[8,4,4,32,128]{4,3,2,1,0:T(8,128)S(1)}, f32[8,4,4,32,128]{4,3,2,1,0:T(8,128)S(1)}, u32[]{:S(2)}, u32[]{:S(2)}) %collective-permute-start) | collective-permute-done | bytes 2097184 | tf_op jit(solution)/shard_map/ppermute | solution.py:155
  10.0 0.2 add_pair.1
  10.2 22.9 %all_to_all.20 = f32[8,512,128]{2,1,0:T(8,128)S(1)} all-to-all(f32[8,512,128]{2,1,0:T(8,128)S(1)} %bitcast.7), channel_id=1, replica_groups={{0,32,8,40,16,48,24,56},{64,96,72,104,80,112,88,120},{128,160,136,168,1..., dimensions={0} | all-to-all | bytes 4194304 | tf_op jit(solution)/shard_map/all_to_all | solution.py:59
  33.1 0.1 reduce_sum.9
  33.2 9.3 %all_to_all.21.parts = f32[4,128,128]{2,1,0:T(8,128)S(1)} all-to-all(f32[4,128,128]{2,1,0:T(8,128)S(1)} %bitcast.10), channel_id=1, replica_groups={{0,2,4,6},{64,66,68,70},{128,130,132,134},{192,194,196,198},{32,34,36,3..., dimensions={0} | all-to-all | bytes 524288 | tf_op jit(solution)/shard_map/all_to_all | solution.py:59
  42.6 12.4 %all_to_all.22.parts = f32[4,128,128]{2,1,0:T(8,128)S(1)} all-to-all(f32[4,128,128]{2,1,0:T(8,128)S(1)} %add_minor.1), channel_id=1, replica_groups={{0,64,128,192},{2,66,130,194},{4,68,132,196},{6,70,134,198},{32,96,160,..., dimensions={0} | all-to-all | bytes 524288 | tf_op jit(solution)/shard_map/all_to_all | solution.py:59
  55.0 16.4 %all_to_all.23.squares = f32[64,1,128]{2,1,0:T(1,128)S(1)} all-to-all(f32[64,1,128]{2,1,0:T(1,128)S(1)} %get-tuple-element.11), channel_id=1, replica_groups={{0,1,2,3,4,5,6,7,8,9,10,11,12,13,14,15,16,17,18,19,20,21,22,23,24,25,26..., dimensions={0} | all-to-all | bytes 65536 | tf_op jit(solution)/shard_map/all_to_all | solution.py:59
  71.4 0.8 %clip.1 = (f32[32,128]{1,0:T(8,128)}, f32[1,1]{1,0:T(1,128)}) custom-call(f32[32,128]{1,0:T(8,128)S(1)} %get-tuple-element.10.unscaled, f32[64,1,128]{2,1,0:T(1,128)S(1)} %all_to_all.23.squares), custom_call_target="tpu_custom_call" | custom-call | tf_op jit(solution)/shard_map/clip/pallas_call | solution.py:145
  (2 shorter events, 0.1 us)
Async XLA Ops:
  2.9 7.1 %collective-permute-start = (f32[8,4,4,32,128]{4,3,2,1,0:T(8,128)S(1)}, f32[8,4,4,32,128]{4,3,2,1,0:T(8,128)S(1)}, u32[]{:S(2)}, u32[]{:S(2)}) collective-permute-start(f32[8,4,4,32,128]{4,3,2,1,0:T(8,128)S(1)} %get-tuple-element.9), channel_id=1, source_target_pairs={{0,1},{1,0},{2,3},{3,2},{4,5},{5,4},{6,7},{7,6},{8,9},{9,8},{10,11... | collective-permute-start | bytes 6291464 | tf_op jit(solution)/shard_map/ppermute | solution.py:155

commit v5 on v4

--- a/solution.py
+++ b/solution.py
@@ -59,26 +59,29 @@
     return lax.all_to_all(blocks, "d", 0, 0, axis_index_groups=groups, tiled=True)
 
 
-def copy_blocks(source, target, sem, partner):
+SPLIT = 2
+
+
+def copy_blocks(source, target, sem, partner, first, count):
     core = (lax.axis_index("d") + partner) % CORES
 
     @pl.when(core == 0)
     def _():
-        for z in range(Z):
-            for x in range(X):
-                pltpu.make_async_copy(source.at[z, x, :, 0], target.at[2 * x + z % 2, :, z // 2], sem).start()
+        for at in range(first, first + count):
+            for high in range(4):
+                z, x = (2 * high + at % 2, at // 2)
+                pltpu.make_async_copy(source.at[z, x, :, 0], target.at[at - first, :, high], sem).start()
 
     @pl.when(core == 1)
     def _():
-        for z in range(Z):
-            for y in range(Y):
-                pltpu.make_async_copy(
-                    source.at[(z + 1) % Z, :, y, 1], target.at[2 * y + z % 2, :, z // 2], sem
-                ).start()
-
-
-def pack_sent(loss_scale, source, sent, scale, sem, scale_sem, scale_smem):
-    copy_blocks(source, sent, sem, 1)
+        for at in range(first, first + count):
+            for high in range(4):
+                z, y = ((2 * high + at % 2 + 1) % Z, at // 2)
+                pltpu.make_async_copy(source.at[z, :, y, 1], target.at[at - first, :, high], sem).start()
+
+
+def pack_first(loss_scale, source, sent, scale, sem, scale_sem, scale_smem):
+    copy_blocks(source, sent, sem, 1, 0, SPLIT)
     copy_scale = pltpu.make_async_copy(loss_scale, scale_smem, scale_sem)
     copy_scale.start()
     copy_scale.wait()
@@ -86,40 +89,52 @@
     pltpu.make_async_copy(sent, sent, sem).wait()
 
 
+def pack_second(source, sent, sem):
+    copy_blocks(source, sent, sem, 1, SPLIT, 8 - SPLIT)
+    pltpu.make_async_copy(sent, sent, sem).wait()
+
+
 def pack_kept(source, kept, sem):
-    copy_blocks(source, kept, sem, 0)
+    copy_blocks(source, kept, sem, 0, 0, 8)
     pltpu.make_async_copy(kept, kept, sem).wait()
 
 
+def vmem_blocks(count):
+    return pltpu.VMEM((count, 4, 4, ROWS, LANES), jnp.float32)
+
+
 def packed(local, loss_scale):
-    blocks = pltpu.VMEM((8, 4, 4, ROWS, LANES), jnp.float32)
     in_hbm, in_vmem = (pl.BlockSpec(memory_space=m) for m in (pltpu.HBM, pltpu.VMEM))
     params = pltpu.CompilerParams(vmem_limit_bytes=4 << 20)
     sem = pltpu.SemaphoreType.DMA
     local = pltpu.with_memory_space_constraint(local, pltpu.HBM)
-    sent, scale = pl.pallas_call(
-        pack_sent,
-        out_shape=(blocks, pltpu.VMEM((1, LANES), jnp.float32)),
+    first, scale = pl.pallas_call(
+        pack_first,
+        out_shape=(vmem_blocks(SPLIT), pltpu.VMEM((1, LANES), jnp.float32)),
         in_specs=[pl.BlockSpec(memory_space=pl.ANY), in_hbm],
         out_specs=(in_vmem, in_vmem),
         scratch_shapes=[sem, sem, pltpu.SMEM((1,), jnp.float32)],
         compiler_params=params,
-        name="pack_sent",
+        name="pack_first",
     )(loss_scale, local)
-    kept = pl.pallas_call(
-        pack_kept,
-        out_shape=blocks,
-        in_specs=[in_hbm],
-        out_specs=in_vmem,
-        scratch_shapes=[sem],
-        compiler_params=params,
-        name="pack_kept",
-    )(local)
-    return sent, kept, scale
-
-
-def add_pair(kept, received, chip):
-    chip[...] = kept[...] + received[...]
+    second, kept = (
+        pl.pallas_call(
+            kernel,
+            out_shape=vmem_blocks(count),
+            in_specs=[in_hbm],
+            out_specs=in_vmem,
+            scratch_shapes=[sem],
+            compiler_params=params,
+            name=kernel.__name__,
+        )(local)
+        for kernel, count in ((pack_second, 8 - SPLIT), (pack_kept, 8))
+    )
+    return first, second, kept, scale
+
+
+def add_pair(kept, first, second, chip):
+    chip[:SPLIT] = kept[:SPLIT] + first[...]
+    chip[SPLIT:] = kept[SPLIT:] + second[...]
 
 
 def add_minor(parts, copies):
@@ -151,9 +166,11 @@
 
 
 def per_device(grads, loss_scale):
-    sent, kept, scale = packed(grads.reshape(Z, X, Y, CORES, ROWS, LANES), loss_scale.reshape(1))
-    received = pltpu.with_memory_space_constraint(lax.ppermute(sent, "d", PAIRS), pltpu.VMEM)
-    chip = called(add_pair, kept, received, out=pltpu.VMEM(kept.shape, jnp.float32), mib=4)
+    first, second, kept, scale = packed(grads.reshape(Z, X, Y, CORES, ROWS, LANES), loss_scale.reshape(1))
+    received = (
+        pltpu.with_memory_space_constraint(lax.ppermute(sent, "d", PAIRS), pltpu.VMEM) for sent in (first, second)
+    )
+    chip = called(add_pair, kept, *received, out=pltpu.VMEM(kept.shape, jnp.float32), mib=4)
     blocks = exchanged(chip.reshape(8, 16 * ROWS, LANES), along_major_and_low())
     blocks = jnp.sum(blocks, axis=0)
     blocks = exchanged(blocks.reshape(4, 4 * ROWS, LANES), along_minor())

time: 72.6 us -> 71.8 us (0.989)
  waiting for transfers between devices: 2.21 us -> 0.34 us
  Pallas kernels: 4.2 us -> 5.14 us
    ppermute x1 -> x2, waiting for transfers between devices: 2.21 us -> 0.34 us  [per_device(): lax.ppermute(sent, 'd', PAIRS)]
    pallas_call x2 -> x3, Pallas kernels: 3.15 us -> 4.09 us  [the longest x2 3 us: packed(): pl.pallas_call(kernel, out_shape=vmem_blocks(count), in_specs=[in_hbm], o...]
    ppermute x1 -> x2, starting transfers between devices: 3.31 us -> 3.43 us  [per_device(): lax.ppermute(sent, 'd', PAIRS)]
  transfers between devices with their start and end apart: 1 -> 2, of which waited for: 1 -> 1; matrix products, arithmetic and copies ran while one was open for 0% -> 0% of each run, Pallas kernels for 2% -> 4%
where the time goes in v5:
time: 71.8 us; the launch traced here: 71.4 us
  blocking collectives  61 us (85%)
  Pallas kernels  5.14 us (7%)
  starting transfers between devices  3.43 us (5%)
  between operations  1.32 us (2%)
    all_to_all x4, blocking collectives, exchanged(): lax.all_to_all(blocks, 'd', 0, 0, axis_index_groups=groups, tiled=True)  61 us
    ppermute x2, starting transfers between devices, per_device(): lax.ppermute(sent, 'd', PAIRS)  3.43 us
    pallas_call x2, Pallas kernels, packed(): pl.pallas_call(kernel, out_shape=vmem_blocks(count), in_specs=[in_hbm], o...  3 us
  transfers between devices with their start and end apart: 2, of which 1 were waited for; matrix products, arithmetic and copies ran while one was open for 0% of the time, Pallas kernels for 4%

profile of v5, /device:TPU:1, one launch (start us, length us, event | category | flops | bytes accessed | tf_op | source)
XLA Modules:
  0.0 71.4 jit_solution(468211762140623880)
XLA Ops:
  0.6 1.4 %pack_second.1 = f32[6,4,4,32,128]{4,3,2,1,0:T(8,128)S(1)} custom-call(f32[8,4,4,2,32,128]{5,4,3,2,1,0:T(8,128)} %bitcast.8), custom_call_target="tpu_custom_call" | custom-call | tf_op jit(solution)/shard_map/pack_second/pallas_call | solution.py:121
  2.0 3.3 %collective-permute-start.1 = (f32[6,4,4,32,128]{4,3,2,1,0:T(8,128)S(1)}, f32[6,4,4,32,128]{4,3,2,1,0:T(8,128)S(1)}, u32[]{:S(2)}, u32[]{:S(2)}) collective-permute-start(f32[6,4,4,32,128]{4,3,2,1,0:T(8,128)S(1)} %pack_second.1), channel_id=1, source_target_pairs={{0,1},{1,0},{2,3},{3,2},{4,5},{5,4},{6,7},{7,6},{8,9},{9,8},{10,11... | collective-permute-start | bytes 4718600 | tf_op jit(solution)/shard_map/ppermute | solution.py:171
  6.0 1.1 %pack_first.1 = (f32[2,4,4,32,128]{4,3,2,1,0:T(8,128)S(1)}, f32[1,128]{1,0:T(1,128)S(1)}) custom-call(f32[1]{0:T(128)} %bitcast.6.loss_scale, f32[8,4,4,2,32,128]{5,4,3,2,1,0:T(8,128)} %bitcast.9), custom_call_target="tpu_custom_call" | custom-call | tf_op jit(solution)/shard_map/pack_first/pallas_call | solution.py:111
  7.1 0.1 collective-permute-start
  7.2 1.6 %pack_kept.1.kept = f32[8,4,4,32,128]{4,3,2,1,0:T(8,128)S(1)} custom-call(f32[8,4,4,2,32,128]{5,4,3,2,1,0:T(8,128)} %bitcast.10), custom_call_target="tpu_custom_call" | custom-call | tf_op jit(solution)/shard_map/pack_kept/pallas_call | solution.py:121
  8.8 0.3 collective-permute-done.first
  9.2 0.0 collective-permute-done.1.second
  9.2 0.2 add_pair.1
  9.4 22.9 %all_to_all.20 = f32[8,512,128]{2,1,0:T(8,128)S(1)} all-to-all(f32[8,512,128]{2,1,0:T(8,128)S(1)} %bitcast.7), channel_id=1, replica_groups={{0,32,8,40,16,48,24,56},{64,96,72,104,80,112,88,120},{128,160,136,168,1..., dimensions={0} | all-to-all | bytes 4194304 | tf_op jit(solution)/shard_map/all_to_all | solution.py:59
  32.3 0.1 reduce_sum.9
  32.4 9.3 %all_to_all.21.parts = f32[4,128,128]{2,1,0:T(8,128)S(1)} all-to-all(f32[4,128,128]{2,1,0:T(8,128)S(1)} %bitcast.11), channel_id=1, replica_groups={{0,2,4,6},{64,66,68,70},{128,130,132,134},{192,194,196,198},{32,34,36,3..., dimensions={0} | all-to-all | bytes 524288 | tf_op jit(solution)/shard_map/all_to_all | solution.py:59
  41.8 12.4 %all_to_all.22.parts = f32[4,128,128]{2,1,0:T(8,128)S(1)} all-to-all(f32[4,128,128]{2,1,0:T(8,128)S(1)} %add_minor.1), channel_id=1, replica_groups={{0,64,128,192},{2,66,130,194},{4,68,132,196},{6,70,134,198},{32,96,160,..., dimensions={0} | all-to-all | bytes 524288 | tf_op jit(solution)/shard_map/all_to_all | solution.py:59
  54.2 16.4 %all_to_all.23.squares = f32[64,1,128]{2,1,0:T(1,128)S(1)} all-to-all(f32[64,1,128]{2,1,0:T(1,128)S(1)} %get-tuple-element.11), channel_id=1, replica_groups={{0,1,2,3,4,5,6,7,8,9,10,11,12,13,14,15,16,17,18,19,20,21,22,23,24,25,26..., dimensions={0} | all-to-all | bytes 65536 | tf_op jit(solution)/shard_map/all_to_all | solution.py:59
  70.6 0.8 %clip.1 = (f32[32,128]{1,0:T(8,128)}, f32[1,1]{1,0:T(1,128)}) custom-call(f32[32,128]{1,0:T(8,128)S(1)} %get-tuple-element.10.unscaled, f32[64,1,128]{2,1,0:T(1,128)S(1)} %all_to_all.23.squares), custom_call_target="tpu_custom_call" | custom-call | tf_op jit(solution)/shard_map/clip/pallas_call | solution.py:160
  (2 shorter events, 0.1 us)
Async XLA Ops:
  2.0 7.1 %collective-permute-start.1 = (f32[6,4,4,32,128]{4,3,2,1,0:T(8,128)S(1)}, f32[6,4,4,32,128]{4,3,2,1,0:T(8,128)S(1)}, u32[]{:S(2)}, u32[]{:S(2)}) collective-permute-start(f32[6,4,4,32,128]{4,3,2,1,0:T(8,128)S(1)} %pack_second.1), channel_id=1, source_target_pairs={{0,1},{1,0},{2,3},{3,2},{4,5},{5,4},{6,7},{7,6},{8,9},{9,8},{10,11... | collective-permute-start | bytes 4718600 | tf_op jit(solution)/shard_map/ppermute | solution.py:171
  7.1 2.0 %collective-permute-start = (f32[2,4,4,32,128]{4,3,2,1,0:T(8,128)S(1)}, f32[2,4,4,32,128]{4,3,2,1,0:T(8,128)S(1)}, u32[]{:S(2)}, u32[]{:S(2)}) collective-permute-start(f32[2,4,4,32,128]{4,3,2,1,0:T(8,128)S(1)} %get-tuple-element.9), channel_id=1, source_target_pairs={{0,1},{1,0},{2,3},{3,2},{4,5},{5,4},{6,7},{7,6},{8,9},{9,8},{10,11... | collective-permute-start | bytes 1572872 | tf_op jit(solution)/shard_map/ppermute | solution.py:171
